TPU v7x, 32 devices: a whole 2x2x4 slice. The times are simulated.
32 devices in a mesh: tp: 8 (over z, y), dp: 4 (over x, core).
Axes of the slice: x: 2, y: 2, z: 4, core: 2. Of those that a mesh axis runs over, the one named last changes fastest.
Arguments:
- normed: bfloat16 [1024, 4096], P(('dp', 'tp')), may hold values from -6 to 6
- cotangent: bfloat16 [1024, 8192], P('dp', 'tp'), may hold values from -1.5 to 1.5
- weight_tiles: bfloat16 [2, 2048, 128, 128], P(None, 'tp'), may hold values from -0.09375 to 0.09375
- slot_tile: int32 [2048], replicated, may hold values from 0 to 2047, as said below
Outputs:
- hidden: bfloat16 [1024, 8192], P('dp', 'tp')
- d_normed: bfloat16 [1024, 4096], P(('dp', 'tp'))
- grad_tiles: float32 [2, 2048, 128, 128], P(None, 'tp', 'dp')
Inputs may be any that keep to these rules, and one draw needn't show every extreme that they name: `slot_tile`: A permutation of 0 to 2047. Position p belongs to owner p // 256 at slot p % 256. Each owner holds 24 to 40 tiles of the tile columns t * 8 to (t + 1) * 8 - 1 of each index t of tp; in every draw some owner holds exactly 40 for some t.
All inputs are finite; a program needn't handle non-finite values.
Results may differ from a plain program's by a relative error of at most 0.018.
Values may be sent and summed in bfloat16 or wider, within the bound.
A program may use at most 128 MiB of HBM per device.

v0:
```python
import jax
import jax.numpy as jnp
from jax import lax
from jax.sharding import PartitionSpec as P

D = 4096
FW = 8192
TILE = 128


def build_lists(slot_tile, groups, owned_count, tile_cols, cols_dev, list_len):
    owned_tiles = slot_tile.reshape(groups, owned_count)
    target = owned_tiles % tile_cols // cols_dev
    matches = (target[:, :, None] == jnp.arange(groups, dtype=jnp.int32)[None, None, :]).astype(
        jnp.int32
    )
    running = jnp.cumsum(matches, axis=1) - 1
    rank_of = jnp.sum(running * matches, axis=2)
    owner_ix = jnp.broadcast_to(jnp.arange(groups, dtype=jnp.int32)[:, None], (groups, owned_count))
    slot_ix = jnp.broadcast_to(
        jnp.arange(owned_count, dtype=jnp.int32)[None, :], (groups, owned_count)
    )
    table = jnp.full((groups, groups, list_len), -1, jnp.int32)
    return table.at[owner_ix, target, rank_of].set(slot_ix, mode="drop")


def incoming_places(in_lists, slot_tile, consumer, tile_cols, cols_dev, owned_count):
    groups = in_lists.shape[0]
    present = in_lists >= 0
    position = jnp.arange(groups, dtype=jnp.int32)[:, None] * owned_count + jnp.maximum(in_lists, 0)
    tile_id = slot_tile[position]
    tile_row = tile_id // tile_cols
    tile_col = tile_id % tile_cols - consumer * cols_dev
    local_idx = tile_row * cols_dev + tile_col
    return (jnp.where(present, local_idx, owned_count), present)


def pick_tiles(source, indices, present):
    limit = source.shape[1] - 1
    picked = source[:, jnp.minimum(indices, limit)]
    mask = present.reshape((1,) + present.shape + (1,) * (source.ndim - 2))
    return jnp.where(mask, picked, jnp.zeros((), source.dtype))


def place_tiles(arrived, places, owned_count):
    flat = arrived.reshape((arrived.shape[0], -1) + arrived.shape[3:])
    empty = jnp.zeros((arrived.shape[0], owned_count) + arrived.shape[3:], arrived.dtype)
    return empty.at[:, places.reshape(-1)].set(flat, mode="drop")


def local(normed, cotangent, weight_tiles, slot_tile):
    tp_size = lax.axis_size("tp")
    consumer = lax.axis_index("tp")
    owned_count = weight_tiles.shape[1]
    tile_size = weight_tiles.shape[2]
    tile_rows = D // TILE
    tile_cols = FW // TILE
    cols_dev = tile_cols // tp_size
    base_count = owned_count // tp_size
    list_len = base_count + base_count // 4
    send_lists = build_lists(slot_tile, tp_size, owned_count, tile_cols, cols_dev, list_len)
    my_lists = lax.dynamic_index_in_dim(send_lists, consumer, 0, keepdims=False)
    out_present = my_lists >= 0
    out_places = jnp.where(out_present, my_lists, owned_count)
    in_lists = lax.dynamic_index_in_dim(send_lists, consumer, 1, keepdims=False)
    in_places, in_present = incoming_places(
        in_lists, slot_tile, consumer, tile_cols, cols_dev, owned_count
    )
    slab_rows = tile_size // lax.axis_size("dp")
    slab_start = lax.axis_index("dp") * slab_rows
    own_rows = lax.dynamic_slice_in_dim(weight_tiles, slab_start, slab_rows, 2)
    outgoing = pick_tiles(own_rows, my_lists, out_present)
    arrived = lax.all_to_all(outgoing, "tp", split_axis=1, concat_axis=1, tiled=True)
    partial_tiles = place_tiles(arrived, in_places, owned_count)
    weight_block = lax.all_gather(partial_tiles, "dp", axis=2, tiled=True)
    weight_block = weight_block.reshape(2, tile_rows, cols_dev, tile_size, tile_size)
    gathered = lax.all_gather(normed, "tp", axis=0, tiled=True)
    group_rows = gathered.shape[0]
    tiled_in = gathered.reshape(group_rows, tile_rows, tile_size)
    both_proj = jnp.einsum(
        "nri,mrcij->nmcj", tiled_in, weight_block, preferred_element_type=jnp.float32
    )
    gate_proj = both_proj[:, 0].reshape(group_rows, -1)
    up_proj = both_proj[:, 1].reshape(group_rows, -1)
    sigmoid_gate = jax.nn.sigmoid(gate_proj)
    act_gate = gate_proj * sigmoid_gate
    hidden = (act_gate * up_proj).astype(jnp.bfloat16)
    cot_full = cotangent.astype(jnp.float32)
    grad_gate = (
        cot_full * up_proj * (sigmoid_gate * (1.0 + gate_proj * (1.0 - sigmoid_gate)))
    ).astype(jnp.bfloat16)
    grad_up = (cot_full * act_gate).astype(jnp.bfloat16)
    grads_in = jnp.stack([grad_gate, grad_up], 1).reshape(group_rows, 2, cols_dev, tile_size)
    term = jnp.einsum("nmcj,mrcij->nri", grads_in, weight_block, preferred_element_type=jnp.float32)
    d_normed = lax.psum_scatter(
        term.reshape(normed.shape[0] * lax.axis_size("tp"), -1).astype(jnp.bfloat16),
        "tp",
        scatter_dimension=0,
        tiled=True,
    )
    partial_value = jnp.einsum(
        "nri,nmcj->mrcij", tiled_in, grads_in, preferred_element_type=jnp.float32
    ).astype(jnp.bfloat16)
    partial_value = partial_value.reshape(2, owned_count, tile_size, tile_size)
    summed = lax.psum_scatter(partial_value, "dp", scatter_dimension=2, tiled=True).astype(
        jnp.float32
    )
    outgoing_grads = pick_tiles(summed, in_places, in_present)
    returned = lax.all_to_all(
        outgoing_grads.astype(jnp.bfloat16), "tp", split_axis=1, concat_axis=1, tiled=True
    ).astype(outgoing_grads.dtype)
    result = place_tiles(returned, out_places, owned_count)
    return (hidden, d_normed, result)


def solution(mesh):
    return jax.shard_map(
        local,
        mesh=mesh,
        in_specs=(P(("dp", "tp"), None), P("dp", "tp"), P(None, "tp", None, None), P()),
        out_specs=(P("dp", "tp"), P(("dp", "tp"), None), P(None, "tp", "dp", None)),
        check_vma=False,
    )
```

profile of v0, /device:TPU:0, one launch (start us, length us, event | category | flops | bytes accessed | tf_op | source)
XLA Modules:
  0.0 721.3 jit_solution(2535239984476430002)
XLA Ops:
  7.2 0.7 reshape.556
  7.9 0.7 reshape.555
  8.6 0.7 and_select_fusion
  9.3 4.5 reduce-window.6
  13.9 0.2 copy.31
  14.2 0.1 fusion.20
  14.3 0.7 and_reduce_fusion
  15.1 0.7 multiply_reduce_fusion
  15.8 8.1 %scatter_custom_fusion.2 = s32[2560]{0:T(1024)S(1)} fusion(s32[2048]{0:T(1024)S(1)} %bitcast.129, s32[2048]{0:T(1024)S(1)} %bitcast.130, s32[]{:T(128)} %constant.86.clone.1), kind=kCustom, calls=%fused_computation.84 | custom fusion | bytes 10244
  23.9 0.1 reshape.568
  24.0 0.1 reshape.581
  24.1 4.9 constant_dynamic-slice_fusion
  29.0 5.9 gather_fusion.1
  34.9 5.3 select_bitcast_fusion
  40.2 7.4 %all-to-all-start = ((bf16[2,8,40,32,128]{4,3,0,2,1:T(8,128)(2,1)}), bf16[2,8,40,32,128]{4,3,0,2,1:T(8,128)(2,1)}, u32[]{:S(2)}, u32[]{:S(2)}) async-start(bf16[2,8,40,32,128]{4,3,0,2,1:T(8,128)(2,1)} %select_bitcast_fusion), calls=%async_computation | async-start | bytes 10485760 | tf_op jit(solution)/shard_map/all_to_all | solution.py:73
  47.7 0.7 all-gather.5.cloned.1.call-update
  48.5 0.1 reshape.573
  48.6 2.2 gather_fusion
  50.9 0.1 gather.16
  51.0 0.1 ge.52
  51.1 137.6 %all-to-all-done = bf16[2,8,40,32,128]{4,3,0,2,1:T(8,128)(2,1)} async-done(((bf16[2,8,40,32,128]{4,3,0,2,1:T(8,128)(2,1)}), bf16[2,8,40,32,128]{4,3,0,2,1:T(8,128)(2,1)}, u32[]{:S(2)}, u32[]{:S(2)}) %all-to-all-start) | async-done | bytes 5242912 | tf_op jit(solution)/shard_map/all_to_all | solution.py:73
  188.7 2.6 broadcast_in_dim.63
  191.3 43.5 %scatter_fusion = bf16[2,256,32,128]{3,2,1,0:T(8,128)(2,1)} fusion(bf16[2,256,32,128]{3,2,1,0:T(8,128)(2,1)} %broadcast_in_dim.63, s32[320]{0:T(512)S(1)} %fusion.42, bf16[320,2,32,128]{3,2,1,0:T(8,128)(2,1)} %bitcast.13), kind=kCustom, calls=%fused_computation.3 | custom fusion | bytes 15729920 | tf_op jit(solution)/shard_map/scatter | solution.py:48
  234.8 0.2 reduce-scatter.5.cloned.1.call-start
  235.0 0.2 copy.38
  235.3 3.3 copy.35
  238.5 100.3 %all-gather.3.cloned.1.call-done = bf16[2,256,128,128]{3,2,1,0:T(8,128)(2,1)} async-done(((bf16[2,256,32,128]{3,2,1,0:T(8,128)(2,1)}), bf16[2,256,128,128]{3,2,1,0:T(8,128)(2,1)}) %all-gather.3.cloned.1.call-update) | async-done | bytes 16777232 | tf_op jit(solution)/shard_map/all_gather | solution.py:75
  338.9 8.1 %convolution_bitcast_fusion = f32[256,2,8,128]{0,3,2,1:T(8,128)S(1)} fusion(bf16[2,32,8,128,128]{4,3,2,1,0:T(8,128)(2,1)} %bitcast.115, bf16[256,32,128,1,1]{0,2,4,1,3:T(8,128)(2,1)S(1)} %bitcast.120), kind=kOutput, calls=%fused_computation.15 | convolution fusion | flops 4294967296 | bytes 20971520 | tf_op jit(solution)/shard_map/nri,mrcij->nmcj/dot_general | solution.py:80
  347.0 0.2 fusion.49
  347.2 1.6 fusion.10
  348.9 0.3 copy.40
  349.1 1.3 copy.39
  350.5 8.1 %convert_bitcast_fusion = bf16[2,32,8,128,128]{3,4,1,2,0:T(8,128)(2,1)} fusion(bf16[256,32,128,1,1]{0,2,1,4,3:T(8,128)(2,1)S(1)} %bitcast.121, bf16[256,1,8,128]{3,0,1,2:T(8,128)(2,1)S(1)} %copy.40, bf16[256,1,8,128]{3,0,1,2:T(8,128)(2,1)S(1)} %copy.39), kind=kOutput, calls=%fused_computation.8 | convolution fusion | flops 4303880192 | bytes 19922944 | tf_op jit(solution)/shard_map/nri,nmcj->mrcij/dot_general | solution.py:101
  358.6 21.2 %copy.45 = bf16[2,32,8,128,128]{4,3,2,1,0:T(8,128)(2,1)} copy(bf16[2,32,8,128,128]{3,4,1,2,0:T(8,128)(2,1)} %convert_bitcast_fusion) | data formatting | bytes 33554432 | tf_op jit(solution)/shard_map/convert_element_type | solution.py:103
  379.8 0.1 reshape.589
  379.9 124.9 %reduce-scatter.5.cloned.1.call-done = bf16[2,256,32,128]{3,2,1,0:T(8,128)(2,1)} async-done(((bf16[2,256,128,128]{3,2,1,0:T(8,128)(2,1)}), bf16[2,256,32,128]{3,2,1,0:T(8,128)(2,1)}) %reduce-scatter.5.cloned.1.call-update) | async-done | bytes 4194320 | tf_op jit(solution)/shard_map/reduce_scatter | solution.py:105
  504.9 5.9 gather_fusion.2
  510.8 6.0 fusion.5
  516.7 5.5 all-to-all-start.1
  522.3 0.3 reduce-scatter.3.cloned.1.call-start
  522.5 18.6 %copy.41 = bf16[32,128,8,128,2]{3,2,4,1,0:T(8,128)(2,1)} copy(bf16[32,128,8,128,2]{3,1,2,0,4:T(8,128)(2,1)} %bitcast.116) | data formatting | bytes 33554432 | tf_op jit(solution)/shard_map/nmcj,mrcij->nri/dot_general | solution.py:94
  541.1 12.6 %fusion.6 = bf16[256,4096]{1,0:T(8,128)(2,1)} fusion(bf16[4096,8,128,2]{2,1,3,0:T(8,128)(2,1)} %bitcast.122, bf16[256,1,8,128]{3,0,1,2:T(8,128)(2,1)S(1)} %copy.40, bf16[256,1,8,128]{3,0,1,2:T(8,128)(2,1)S(1)} %copy.39), kind=kOutput, calls=%fused_computation.14 | convolution fusion | flops 4296540160 | bytes 19922944 | tf_op jit(solution)/shard_map/nmcj,mrcij->nri/dot_general | solution.py:94
  553.7 0.1 squeeze.6
  553.8 1.0 copy.46
  554.8 99.9 %all-to-all-done.1 = bf16[2,8,40,32,128]{4,3,0,2,1:T(8,128)(2,1)} async-done(((bf16[2,8,40,32,128]{4,3,0,2,1:T(8,128)(2,1)}), bf16[2,8,40,32,128]{4,3,0,2,1:T(8,128)(2,1)}, u32[]{:S(2)}, u32[]{:S(2)}) %all-to-all-start.1) | async-done | bytes 5242912 | tf_op jit(solution)/shard_map/all_to_all | solution.py:109
  654.7 8.0 %convert_bitcast_fusion.1 = f32[320,2,32,128]{3,2,1,0:T(8,128)} fusion(bf16[2,8,40,32,128]{4,3,0,2,1:T(8,128)(2,1)} %all-to-all-done.1), kind=kLoop, calls=%fused_computation.9 | loop fusion | flops 2621440 | bytes 15728640 | tf_op jit(solution)/shard_map/reshape | solution.py:46
  662.7 4.5 broadcast_in_dim.71
  667.2 47.6 %scatter_fusion.1 = f32[2,256,32,128]{3,2,1,0:T(8,128)} fusion(f32[2,256,32,128]{3,2,1,0:T(8,128)} %broadcast_in_dim.71, s32[320]{0:T(512)S(1)} %fusion.43, f32[320,2,32,128]{3,2,1,0:T(8,128)} %convert_bitcast_fusion.1), kind=kCustom, calls=%fused_computation.4 | custom fusion | bytes 31458560 | tf_op jit(solution)/shard_map/scatter | solution.py:48
  (37 shorter events, 0.6 us)
Async XLA Ops:
  40.2 8.4 %copy-start = (s32[2048]{0:T(1024)S(1)}, s32[2048]{0:T(1024)}, u32[]{:S(2)}) copy-start(s32[2048]{0:T(1024)} %param.7) | copy-start | bytes 24580
  40.2 148.5 %all-to-all-start = ((bf16[2,8,40,32,128]{4,3,0,2,1:T(8,128)(2,1)}), bf16[2,8,40,32,128]{4,3,0,2,1:T(8,128)(2,1)}, u32[]{:S(2)}, u32[]{:S(2)}) async-start(bf16[2,8,40,32,128]{4,3,0,2,1:T(8,128)(2,1)} %select_bitcast_fusion), calls=%async_computation | async-start | bytes 10485760 | tf_op jit(solution)/shard_map/all_to_all | solution.py:73
  47.6 187.6 %all-gather.5.cloned.1.call-start = ((), (), s32[]{:S(2)}) async-start(), calls=%async_computation.5 | async-start | bytes 2359296 | tf_op jit(solution)/shard_map/all_gather | solution.py:77
  48.4 290.5 %all-gather.3.cloned.1.call-start = ((), (), s32[]{:S(2)}) async-start(), calls=%async_computation.4 | async-start | bytes 20971520 | tf_op jit(solution)/shard_map/all_gather | solution.py:75
  191.3 43.7 %copy-start.2 = (bf16[256,1024]{1,0:T(8,128)(2,1)S(1)}, bf16[256,1024]{1,0:T(8,128)(2,1)}, u32[]{:S(2)}) copy-start(bf16[256,1024]{1,0:T(8,128)(2,1)} %param.5) | copy-start | bytes 1572868
  234.8 270.1 %reduce-scatter.5.cloned.1.call-start = ((), (), s32[]{:S(2)}) async-start(), calls=%async_computation.7 | async-start | bytes 20971520 | tf_op jit(solution)/shard_map/reduce_scatter | solution.py:105
  516.7 138.0 %all-to-all-start.1 = ((bf16[2,8,40,32,128]{4,3,0,2,1:T(8,128)(2,1)}), bf16[2,8,40,32,128]{4,3,0,2,1:T(8,128)(2,1)}, u32[]{:S(2)}, u32[]{:S(2)}) async-start(bf16[2,8,40,32,128]{4,3,0,2,1:T(8,128)(2,1)} %fusion.5), calls=%async_computation.3 | async-start | bytes 10485760 | tf_op jit(solution)/shard_map/all_to_all | solution.py:109
  522.3 192.5 %reduce-scatter.3.cloned.1.call-start = ((), (), s32[]{:S(2)}) async-start(), calls=%async_computation.6 | async-start | bytes 2359296 | tf_op jit(solution)/shard_map/reduce_scatter | solution.py:95
  541.1 12.7 %copy-start.1 = (bf16[256,1024]{0,1:T(8,128)(2,1)S(1)}, bf16[256,1024]{0,1:T(8,128)(2,1)}, u32[]{:S(2)}) copy-start(bf16[256,1024]{0,1:T(8,128)(2,1)} %get-tuple-element.16) | copy-start | bytes 1572868
Sparse Core Ops, SparseCore 0:
  50.6 119.8 all-gather.4
  234.9 103.9 all-gather.2
  380.0 124.8 reduce-scatter.4
  553.8 121.1 reduce-scatter.2
where the time goes:
time: 724 us; the launch traced here: 721 us
  waiting for transfers between devices  464 us (64%)
  local copies, waits for them, and re-layouts  173 us (24%)
  matrix products  28.8 us (4%)
  other arithmetic  28.1 us (4%)
  between operations  14 us (2%)
  starting transfers between devices  13.5 us (2%)
    all_to_all x1, waiting for transfers between devices, local(): lax.all_to_all(outgoing, 'tp', split_axis=1, concat_axis=1, tiled=True)  138 us
    reduce_scatter x1, waiting for transfers between devices, local(): lax.psum_scatter(partial_value, 'dp', scatter_dimension=2, tiled=True)  125 us
    all_gather x1, waiting for transfers between devices, local(): weight_block = lax.all_gather(partial_tiles, 'dp', axis=2, tiled=True)  100 us
    all_to_all x1, waiting for transfers between devices, local(): lax.all_to_all(outgoing_grads.astype(jnp.bfloat16), 'tp', split_axis=1, c...  99.9 us
    scatter x2, local copies, waits for them, and re-layouts, place_tiles(): return empty.at[:, places.reshape(-1)].set(flat, mode='drop')  91.1 us
    convert_element_type x1, local copies, waits for them, and re-layouts, local(): partial_value = jnp.einsum('nri,nmcj->mrcij', tiled_in, grads_in, preferr...  21.2 us
    dot_general x1, local copies, waits for them, and re-layouts, local(): jnp.einsum('nmcj,mrcij->nri', grads_in, weight_block, preferred_element_t...  18.6 us
  transfers between devices with their start and end apart: 6, of which 4 were waited for; matrix products, arithmetic and copies ran while one was open for 20% of the time, Pallas kernels for 0%

commit v1 on v0

--- a/solution.py
+++ b/solution.py
@@ -72,7 +72,12 @@
     outgoing = pick_tiles(own_rows, my_lists, out_present)
     arrived = lax.all_to_all(outgoing, "tp", split_axis=1, concat_axis=1, tiled=True)
     partial_tiles = place_tiles(arrived, in_places, owned_count)
-    weight_block = lax.all_gather(partial_tiles, "dp", axis=2, tiled=True)
+    ring = [partial_tiles]
+    for hop in range(3):
+        ring.append(lax.ppermute(ring[-1], "dp", [(dev, (dev + 1) % 4) for dev in range(4)]))
+    weight_block = jnp.roll(
+        jnp.concatenate(ring[::-1], axis=2), (lax.axis_index("dp") + 1) * ring[0].shape[2], axis=2
+    )
     weight_block = weight_block.reshape(2, tile_rows, cols_dev, tile_size, tile_size)
     gathered = lax.all_gather(normed, "tp", axis=0, tiled=True)
     group_rows = gathered.shape[0]

time: 724 us -> 781 us (1.079)
  local copies, waits for them, and re-layouts: 173 us -> 217 us
  waiting for transfers between devices: 464 us -> 481 us
    all_gather x1 -> x0, waiting for transfers between devices: 100 us -> none  [local(): weight_block = lax.all_gather(partial_tiles, 'dp', axis=2, tiled=True)]
    ppermute x0 -> x3, waiting for transfers between devices: none -> 96.2 us  [local(): lax.ppermute(ring[-1], 'dp', [(dev, (dev + 1) % 4) for dev in range(4)])]
    all_gather x1, waiting for transfers between devices: 0.02 us -> 48 us  [local(): gathered = lax.all_gather(normed, 'tp', axis=0, tiled=True)]
    unnamed x12 -> x27, local copies, waits for them, and re-layouts: 9.29 us -> 40.9 us
    all_to_all x1, waiting for transfers between devices: 138 us -> 113 us  [local(): lax.all_to_all(outgoing, 'tp', split_axis=1, concat_axis=1, tiled=True)]
    dynamic_slice x0 -> x1, local copies, waits for them, and re-layouts: none -> 8.8 us  [local(): jnp.roll(jnp.concatenate(ring[::-1], axis=2), (lax.axis_index('dp') + 1)...]
  transfers between devices with their start and end apart: 6 -> 8, of which waited for: 4 -> 6; matrix products, arithmetic and copies ran while one was open for 20% -> 13% of each run, Pallas kernels for 0% -> 0%
where the time goes in v1:
time: 781 us; the launch traced here: 778 us
  waiting for transfers between devices  481 us (62%)
  local copies, waits for them, and re-layouts  217 us (28%)
  other arithmetic  28.1 us (4%)
  matrix products  25.5 us (3%)
  between operations  14 us (2%)
  starting transfers between devices  13.3 us (2%)
    reduce_scatter x1, waiting for transfers between devices, local(): lax.psum_scatter(partial_value, 'dp', scatter_dimension=2, tiled=True)  123 us
    all_to_all x1, waiting for transfers between devices, local(): lax.all_to_all(outgoing, 'tp', split_axis=1, concat_axis=1, tiled=True)  113 us
    all_to_all x1, waiting for transfers between devices, local(): lax.all_to_all(outgoing_grads.astype(jnp.bfloat16), 'tp', split_axis=1, c...  99.8 us
    ppermute x3, waiting for transfers between devices, local(): lax.ppermute(ring[-1], 'dp', [(dev, (dev + 1) % 4) for dev in range(4)])  96.2 us
    scatter x2, local copies, waits for them, and re-layouts, place_tiles(): return empty.at[:, places.reshape(-1)].set(flat, mode='drop')  91.1 us
    all_gather x1, waiting for transfers between devices, local(): gathered = lax.all_gather(normed, 'tp', axis=0, tiled=True)  48 us
    unnamed x27, local copies, waits for them, and re-layouts  40.9 us
    convert_element_type x1, local copies, waits for them, and re-layouts, local(): partial_value = jnp.einsum('nri,nmcj->mrcij', tiled_in, grads_in, preferr...  21.2 us
  transfers between devices with their start and end apart: 8, of which 6 were waited for; matrix products, arithmetic and copies ran while one was open for 13% of the time, Pallas kernels for 0%

profile of v1, /device:TPU:0, one launch (start us, length us, event | category | flops | bytes accessed | tf_op | source)
XLA Modules:
  0.0 778.3 jit_solution(12381843510636720960)
XLA Ops:
  7.2 0.7 reshape.556
  7.9 0.7 reshape.555
  8.6 0.7 and_select_fusion
  9.3 4.5 reduce-window.6
  14.3 0.7 multiply_reduce_fusion
  15.1 0.7 and_reduce_fusion
  15.8 8.1 %scatter_custom_fusion.2 = s32[2560]{0:T(1024)S(1)} fusion(s32[2048]{0:T(1024)S(1)} %bitcast.129, s32[2048]{0:T(1024)S(1)} %bitcast.130, s32[]{:T(128)} %constant.105.clone.1), kind=kCustom, calls=%fused_computation.92 | custom fusion | bytes 10244
  24.1 4.9 constant_dynamic-slice_fusion.1
  29.0 5.9 gather_fusion.1
  34.9 5.3 select_bitcast_fusion
  40.2 7.4 all-to-all-start
  47.9 2.2 gather_fusion
  50.4 113.0 %all-to-all-done = bf16[2,8,40,32,128]{4,3,0,2,1:T(8,128)(2,1)} async-done(((bf16[2,8,40,32,128]{4,3,0,2,1:T(8,128)(2,1)}), bf16[2,8,40,32,128]{4,3,0,2,1:T(8,128)(2,1)}, u32[]{:S(2)}, u32[]{:S(2)}) %all-to-all-start) | async-done | bytes 5242912 | tf_op jit(solution)/shard_map/all_to_all | solution.py:73
  163.4 2.6 broadcast_in_dim.63
  165.9 43.5 %scatter_fusion = bf16[2,256,32,128]{3,2,1,0:T(8,128)(2,1)} fusion(bf16[2,256,32,128]{3,2,1,0:T(8,128)(2,1)} %broadcast_in_dim.63, s32[320]{0:T(512)S(1)} %fusion.42, bf16[320,2,32,128]{3,2,1,0:T(8,128)(2,1)} %bitcast.13), kind=kCustom, calls=%fused_computation.3 | custom fusion | bytes 15729920 | tf_op jit(solution)/shard_map/scatter | solution.py:48
  209.4 48.1 %collective-permute-done = bf16[2,256,32,128]{3,2,1,0:T(8,128)(2,1)S(1)} collective-permute-done((bf16[2,256,32,128]{3,2,1,0:T(8,128)(2,1)}, bf16[2,256,32,128]{3,2,1,0:T(8,128)(2,1)S(1)}, u32[]{:S(2)}, u32[]{:S(2)}) %collective-permute-start) | collective-permute-done | bytes 4194336 | tf_op jit(solution)/shard_map/ppermute | solution.py:77
  257.6 1.9 copy-done.3
  259.5 48.0 %collective-permute-done.1 = bf16[2,256,32,128]{3,2,1,0:T(8,128)(2,1)} collective-permute-done((bf16[2,256,32,128]{3,2,1,0:T(8,128)(2,1)S(1)}, bf16[2,256,32,128]{3,2,1,0:T(8,128)(2,1)}, u32[]{:S(2)}, u32[]{:S(2)}) %collective-permute-start.1) | collective-permute-done | bytes 4194336 | tf_op jit(solution)/shard_map/ppermute | solution.py:77
  308.0 48.0 %all-gather.2.cloned.1.call-done = bf16[256,4096]{1,0:T(8,128)(2,1)} async-done(((bf16[32,4096]{1,0:T(8,128)(2,1)}), bf16[256,4096]{1,0:T(8,128)(2,1)}) %all-gather.2.cloned.1.call-update) | async-done | bytes 2097168 | tf_op jit(solution)/shard_map/all_gather | solution.py:82
  356.1 3.3 copy.35
  359.3 4.9 constant_dynamic-update-slice_fusion.7
  364.3 5.1 constant_dynamic-update-slice_fusion.6
  369.4 2.8 constant_dynamic-update-slice_fusion.5
  372.1 0.7 copy-done.2
  372.9 2.7 constant_dynamic-update-slice_fusion.4
  375.6 4.9 constant_dynamic-update-slice_fusion.3
  380.5 5.0 constant_dynamic-update-slice_fusion.2
  385.5 2.7 constant_dynamic-update-slice_fusion.1
  388.2 2.8 constant_dynamic-update-slice_fusion
  391.0 8.8 %constant_dynamic-slice_fusion = bf16[2,256,128,128]{3,2,1,0:T(8,128)(2,1)S(1)} fusion(bf16[2,256,256,128]{3,2,1,0:T(8,128)(2,1)} %constant_dynamic-update-slice_fusion, s32[]{:T(128)S(6)} %select_n.238), kind=kLoop, calls=%fused_computation.124 | loop fusion | bytes 33554436 | tf_op jit(solution)/shard_map/jit(_roll_dynamic)/dynamic_slice | solution.py:78
  399.8 4.8 convolution_bitcast_fusion
  404.6 0.9 copy-done.1
  405.7 1.6 fusion.10
  407.3 0.3 copy.39
  407.6 1.3 copy.40
  408.9 8.1 %convert_bitcast_fusion = bf16[2,32,8,128,128]{3,4,1,2,0:T(8,128)(2,1)} fusion(bf16[256,32,128,1,1]{0,2,1,4,3:T(8,128)(2,1)S(1)} %bitcast.121, bf16[256,1,8,128]{3,0,1,2:T(8,128)(2,1)S(1)} %copy.40, bf16[256,1,8,128]{3,0,1,2:T(8,128)(2,1)S(1)} %copy.39), kind=kOutput, calls=%fused_computation.8 | convolution fusion | flops 4303880192 | bytes 19922944 | tf_op jit(solution)/shard_map/nri,nmcj->mrcij/dot_general | solution.py:106
  417.0 21.2 %copy.45 = bf16[2,32,8,128,128]{4,3,2,1,0:T(8,128)(2,1)} copy(bf16[2,32,8,128,128]{3,4,1,2,0:T(8,128)(2,1)} %convert_bitcast_fusion) | data formatting | bytes 33554432 | tf_op jit(solution)/shard_map/convert_element_type | solution.py:108
  438.4 123.5 %reduce-scatter.5.cloned.1.call-done = bf16[2,256,32,128]{3,2,1,0:T(8,128)(2,1)} async-done(((bf16[2,256,128,128]{3,2,1,0:T(8,128)(2,1)}), bf16[2,256,32,128]{3,2,1,0:T(8,128)(2,1)}) %reduce-scatter.5.cloned.1.call-update) | async-done | bytes 4194320 | tf_op jit(solution)/shard_map/reduce_scatter | solution.py:110
  561.8 5.9 gather_fusion.2
  567.7 6.0 fusion.5
  573.7 5.5 all-to-all-start.1
  579.3 18.8 %copy.41 = bf16[32,128,8,128,2]{3,2,4,1,0:T(8,128)(2,1)} copy(bf16[32,128,8,128,2]{3,1,2,0,4:T(8,128)(2,1)} %bitcast.116) | data formatting | bytes 33554432 | tf_op jit(solution)/shard_map/nmcj,mrcij->nri/dot_general | solution.py:99
  598.1 12.6 %fusion.6 = bf16[256,4096]{1,0:T(8,128)(2,1)} fusion(bf16[4096,8,128,2]{2,1,3,0:T(8,128)(2,1)} %bitcast.122, bf16[256,1,8,128]{3,0,1,2:T(8,128)(2,1)S(1)} %copy.40, bf16[256,1,8,128]{3,0,1,2:T(8,128)(2,1)S(1)} %copy.39), kind=kOutput, calls=%fused_computation.14 | convolution fusion | flops 4296540160 | bytes 19922944 | tf_op jit(solution)/shard_map/nmcj,mrcij->nri/dot_general | solution.py:99
  610.9 1.0 copy.46
  611.9 99.8 %all-to-all-done.1 = bf16[2,8,40,32,128]{4,3,0,2,1:T(8,128)(2,1)} async-done(((bf16[2,8,40,32,128]{4,3,0,2,1:T(8,128)(2,1)}), bf16[2,8,40,32,128]{4,3,0,2,1:T(8,128)(2,1)}, u32[]{:S(2)}, u32[]{:S(2)}) %all-to-all-start.1) | async-done | bytes 5242912 | tf_op jit(solution)/shard_map/all_to_all | solution.py:114
  711.7 8.0 %convert_bitcast_fusion.1 = f32[320,2,32,128]{3,2,1,0:T(8,128)} fusion(bf16[2,8,40,32,128]{4,3,0,2,1:T(8,128)(2,1)} %all-to-all-done.1), kind=kLoop, calls=%fused_computation.9 | loop fusion | flops 2621440 | bytes 15728640 | tf_op jit(solution)/shard_map/reshape | solution.py:46
  719.7 4.5 broadcast_in_dim.71
  724.1 47.6 %scatter_fusion.1 = f32[2,256,32,128]{3,2,1,0:T(8,128)} fusion(f32[2,256,32,128]{3,2,1,0:T(8,128)} %broadcast_in_dim.71, s32[320]{0:T(512)S(1)} %fusion.43, f32[320,2,32,128]{3,2,1,0:T(8,128)} %convert_bitcast_fusion.1), kind=kCustom, calls=%fused_computation.4 | custom fusion | bytes 31458560 | tf_op jit(solution)/shard_map/scatter | solution.py:48
  (57 shorter events, 2.0 us)
Async XLA Ops:
  40.2 7.7 copy-start
  40.2 123.2 %all-to-all-start = ((bf16[2,8,40,32,128]{4,3,0,2,1:T(8,128)(2,1)}), bf16[2,8,40,32,128]{4,3,0,2,1:T(8,128)(2,1)}, u32[]{:S(2)}, u32[]{:S(2)}) async-start(bf16[2,8,40,32,128]{4,3,0,2,1:T(8,128)(2,1)} %select_bitcast_fusion), calls=%async_computation | async-start | bytes 10485760 | tf_op jit(solution)/shard_map/all_to_all | solution.py:73
  47.6 308.4 %all-gather.2.cloned.1.call-start = ((), (), s32[]{:S(2)}) async-start(), calls=%async_computation.4 | async-start | bytes 2359296 | tf_op jit(solution)/shard_map/all_gather | solution.py:82
  165.9 141.9 %copy-start.6 = (bf16[256,1024]{1,0:T(8,128)(2,1)S(1)}, bf16[256,1024]{1,0:T(8,128)(2,1)}, u32[]{:S(2)}) copy-start(bf16[256,1024]{1,0:T(8,128)(2,1)} %param.5) | copy-start | bytes 1572868
  209.4 48.1 %collective-permute-start = (bf16[2,256,32,128]{3,2,1,0:T(8,128)(2,1)}, bf16[2,256,32,128]{3,2,1,0:T(8,128)(2,1)S(1)}, u32[]{:S(2)}, u32[]{:S(2)}) collective-permute-start(bf16[2,256,32,128]{3,2,1,0:T(8,128)(2,1)} %scatter_fusion), channel_id=1, source_target_pairs={{0,1},{1,2},{2,3},{3,0},{4,5},{5,6},{6,7},{7,4},{8,9},{9,10},{10,1... | collective-permute-start | bytes 12582920 | tf_op jit(solution)/shard_map/ppermute | solution.py:77
  257.6 1.9 copy-start.3
  259.5 48.0 %collective-permute-start.1 = (bf16[2,256,32,128]{3,2,1,0:T(8,128)(2,1)S(1)}, bf16[2,256,32,128]{3,2,1,0:T(8,128)(2,1)}, u32[]{:S(2)}, u32[]{:S(2)}) collective-permute-start(bf16[2,256,32,128]{3,2,1,0:T(8,128)(2,1)S(1)} %collective-permute-done), channel_id=1, source_target_pairs={{0,1},{1,2},{2,3},{3,0},{4,5},{5,6},{6,7},{7,4},{8,9},{9,10},{10,1... | collective-permute-start | bytes 12582920 | tf_op jit(solution)/shard_map/ppermute | solution.py:77
  307.5 51.8 %collective-permute-start.2 = (bf16[2,256,32,128]{3,2,1,0:T(8,128)(2,1)}, bf16[2,256,32,128]{3,2,1,0:T(8,128)(2,1)}, u32[]{:S(2)}, u32[]{:S(2)}) collective-permute-start(bf16[2,256,32,128]{3,2,1,0:T(8,128)(2,1)} %collective-permute-done.1), channel_id=1, source_target_pairs={{0,1},{1,2},{2,3},{3,0},{4,5},{5,6},{6,7},{7,4},{8,9},{9,10},{10,1... | collective-permute-start | bytes 12582920 | tf_op jit(solution)/shard_map/ppermute | solution.py:77
  307.6 254.3 %reduce-scatter.5.cloned.1.call-start = ((), (), s32[]{:S(2)}) async-start(), calls=%async_computation.6 | async-start | bytes 20971520 | tf_op jit(solution)/shard_map/reduce_scatter | solution.py:110
  364.3 5.1 copy-start.4
  369.4 3.5 copy-start.2
  399.8 5.7 copy-start.1
  573.7 138.0 %all-to-all-start.1 = ((bf16[2,8,40,32,128]{4,3,0,2,1:T(8,128)(2,1)}), bf16[2,8,40,32,128]{4,3,0,2,1:T(8,128)(2,1)}, u32[]{:S(2)}, u32[]{:S(2)}) async-start(bf16[2,8,40,32,128]{4,3,0,2,1:T(8,128)(2,1)} %fusion.5), calls=%async_computation.3 | async-start | bytes 10485760 | tf_op jit(solution)/shard_map/all_to_all | solution.py:114
  579.2 192.5 %reduce-scatter.3.cloned.1.call-start = ((), (), s32[]{:S(2)}) async-start(), calls=%async_computation.5 | async-start | bytes 2359296 | tf_op jit(solution)/shard_map/reduce_scatter | solution.py:100
  598.1 12.7 %copy-start.5 = (bf16[256,1024]{0,1:T(8,128)(2,1)S(1)}, bf16[256,1024]{0,1:T(8,128)(2,1)}, u32[]{:S(2)}) copy-start(bf16[256,1024]{0,1:T(8,128)(2,1)} %get-tuple-element.16) | copy-start | bytes 1572868
Sparse Core Ops, SparseCore 0:
  307.7 48.3 all-gather.1
  438.4 123.3 reduce-scatter.4
  610.9 135.1 reduce-scatter.2
